TPU v7x, 16 devices: a 4x2x1 block of a 4x4x4 slice. The times are simulated.
16 devices in a mesh: dp: 2 (over y, z), sp: 8 (over x, core).
Axes of the slice: x: 4, y: 2, z: 1, core: 2. Of those that a mesh axis runs over, the one named last changes fastest.
The devices are a block of a 4x4x4 slice.
Arguments:
- q: bfloat16 [64, 32, 160], P('dp'), parts along dimension 0
- k: bfloat16 [64, 8192, 8, 160], P('dp', 'sp'), parts along dimension 0
- v: bfloat16 [64, 8192, 8, 160], P('dp', 'sp'), parts along dimension 0
Outputs:
- q: bfloat16 [64, 32, 160], P('dp'), parts along dimension 0
There are 2 independent parts. A program takes and returns all parts, laid end to end along the dimension named above; each array names one.
All inputs are finite; a program needn't handle non-finite values.
Results may differ from a plain program's by a relative error of at most 0.012.
Values are sent between devices in bfloat16 or wider.
A program may use at most 1.5 GiB of HBM per device.

v0:
```python
import jax
import jax.numpy as jnp
from jax import lax
from jax.sharding import PartitionSpec as P


def einsum(form, a, b):
    return jnp.einsum(form, a.astype(jnp.float32), b.astype(jnp.float32))


def part_of(q, k, v):
    grouped = q.reshape(q.shape[0], k.shape[2], -1, q.shape[2])
    scores = einsum("bgsd,bugd->bgsu", grouped, k) * q.shape[2] ** -0.5
    high = jnp.max(scores, -1, keepdims=True)
    weights = jnp.exp(scores - high)
    seen = einsum("bgsu,bugd->bgsd", weights.astype(jnp.bfloat16), v)
    return jnp.concatenate([seen, jnp.sum(weights, -1, keepdims=True), high], -1)


def together(parts):
    seen, total, high = parts[..., :-2], parts[..., -2:-1], parts[..., -1:]
    scale = jnp.exp(high - jnp.max(high, 0))
    return (jnp.sum(seen * scale, 0) / jnp.sum(total * scale, 0)).astype(jnp.bfloat16)


def solution(mesh):
    def step(q, k, v):
        return together(lax.all_gather(part_of(q, k, v), "sp")).reshape(q.shape)

    return jax.shard_map(
        step,
        mesh=mesh,
        in_specs=(P("dp", None, None), P("dp", "sp", None, None), P("dp", "sp", None, None)),
        out_specs=P("dp", None, None),
        check_vma=False,
    )
```

profile of v0, /device:TPU:113, one launch (start us, length us, event | category | flops | bytes accessed | tf_op | source)
XLA Modules:
  0.0 157.3 jit_solution(13424974497194115744)
XLA Ops:
  6.5 0.0 all-gather.3.cloned.1.call-start
  6.6 1.2 reshape.15
  7.8 30.1 %multiply_reduce_fusion = (f32[32,8,4]{2,1,0:T(8,128)S(1)}, f32[32,8,4,1024]{3,2,1,0:T(4,128)}) fusion(bf16[32,8,4,160]{3,2,1,0:T(4,128)(2,1)S(1)} %reshape.15, bf16[32,1024,8,160]{1,3,2,0:T(8,128)(2,1)} %param.4), kind=kOutput, calls=%fused_computation.3 | convolution fusion | flops 337640448 | bytes 88412160 | tf_op jit(solution)/shard_map/bgsd,bugd->bgsu/dot_general | solution.py:8
  37.8 3.6 %fusion.1 = f32[32,8,4]{2,1,0:T(8,128)S(1)} fusion(f32[32,8,4,1024]{3,2,1,0:T(4,128)} %get-tuple-element.11, f32[32,8,4]{2,1,0:T(8,128)S(1)} %get-tuple-element.10), kind=kLoop, calls=%fused_computation.4 | loop fusion | flops 3144704 | bytes 4202496 | tf_op jit(solution)/shard_map/reduce_sum | solution.py:17
  41.4 32.0 %fusion.3 = f32[32,8,4,160]{3,2,1,0:T(4,128)S(1)} fusion(bf16[32,1024,8,160]{1,3,2,0:T(8,128)(2,1)} %param.5, f32[32,8,4,1024]{3,2,1,0:T(4,128)} %get-tuple-element.11, f32[32,8,4]{2,1,0:T(8,128)S(1)} %get-tuple-element.10), kind=kOutput, calls=%fused_computation.6 | convolution fusion | flops 338690048 | bytes 88739840 | tf_op jit(solution)/shard_map/bgsu,bugd->bgsd/dot_general | solution.py:8
  73.5 1.7 %copy.51 = f32[32,8,4,1]{3,2,1,0:T(4,128)S(1)} copy(f32[32,8,4,1]{2,1,0,3:T(8,128)S(1)} %bitcast.16) | data formatting | bytes 8192 | tf_op jit(solution)/shard_map/broadcast_in_dim | solution.py:17
  75.2 1.7 %copy.52 = f32[32,8,4,1]{3,2,1,0:T(4,128)S(1)} copy(f32[32,8,4,1]{2,1,0,3:T(8,128)S(1)} %bitcast.15) | data formatting | bytes 8192 | tf_op jit(solution)/shard_map/broadcast_in_dim | solution.py:14
  76.8 0.7 pad_maximum_fusion
  77.5 1.3 copy.53
  78.8 0.1 all-gather.3.cloned.1.call-update
  78.8 48.9 %all-gather.3.cloned.1.call-done = f32[256,8,4,162]{3,1,2,0:T(8,128)} async-done(((f32[32,8,4,162]{3,1,2,0:T(8,128)}), f32[256,8,4,162]{3,1,2,0:T(8,128)}) %all-gather.3.cloned.1.call-update) | async-done | bytes 5308432 | tf_op jit(solution)/shard_map/all_gather | solution.py:28
  127.7 8.9 %fusion.10 = (f32[8,32,8,4,1]{4,2,3,1,0:T(8,128)}, f32[32,8,4]{1,2,0:T(4,128)S(1)}, f32[8,32,8,4,1]{4,2,3,1,0:T(8,128)}) fusion(f32[8,32,8,4,162]{4,2,3,1,0:T(8,128)} %bitcast.13), kind=kLoop, calls=%fused_computation.17 | loop fusion | flops 7168 | bytes 135168 | tf_op jit(solution)/shard_map/slice | solution.py:21
  136.6 3.6 %copy.65 = f32[8,32,8,4,1]{1,2,4,3,0:T(8,128)S(1)} copy(f32[8,32,8,4,1]{4,2,3,1,0:T(8,128)} %get-tuple-element.5) | data formatting | bytes 65536
  140.2 0.1 copy.66
  140.3 3.7 %copy.64 = f32[8,32,8,4,1]{1,2,4,3,0:T(8,128)S(1)} copy(f32[8,32,8,4,1]{4,2,3,1,0:T(8,128)} %get-tuple-element.7) | data formatting | bytes 65536
  144.1 0.2 copy.55
  144.4 4.2 %fusion = f32[32,8,4,160]{3,1,2,0:T(8,128)S(1)} fusion(f32[8,32,8,4,162]{4,2,3,1,0:T(8,128)} %bitcast.14, f32[8,32,8,4]{2,3,1,0:T(4,128)S(1)} %copy.55), kind=kLoop, calls=%fused_computation.1 | loop fusion | flops 2457600 | bytes 5931008 | tf_op jit(solution)/shard_map/reduce_sum | solution.py:23
  148.5 0.6 copy.56
  149.1 0.2 fusion.7
  149.4 1.1 copy.59
  (2 shorter events, 0.0 us)
Async XLA Ops:
  6.5 121.2 %all-gather.3.cloned.1.call-start = ((), (), s32[]{:S(2)}) async-start(), calls=%async_computation | async-start | bytes 9437184 | tf_op jit(solution)/shard_map/all_gather | solution.py:28
Sparse Core Ops, SparseCore 0:
  78.9 48.7 all-gather.2
where the time goes:
time: 158 us; the launch traced here: 157 us
  matrix products  62.1 us (39%)
  waiting for transfers between devices  49 us (31%)
  other arithmetic  17.6 us (11%)
  local copies, waits for them, and re-layouts  15.2 us (10%)
  between operations  13.5 us (9%)
    dot_general x2, matrix products, einsum(): return jnp.einsum(form, a.astype(jnp.float32), b.astype(jnp.float32))  62.1 us
    all_gather x1, waiting for transfers between devices, step(): return together(lax.all_gather(part_of(q, k, v), 'sp')).reshape(q.shape)  48.9 us
    slice x1, other arithmetic, together(): seen, total, high = (parts[..., :-2], parts[..., -2:-1], parts[..., -1:])  8.92 us
    unnamed x3, local copies, waits for them, and re-layouts  7.41 us
    reduce_sum x1, other arithmetic, together(): jnp.sum(seen * scale, 0) / jnp.sum(total * scale, 0)  4.16 us
    reduce_sum x1, other arithmetic, part_of(): jnp.sum(weights, -1, keepdims=True)  3.62 us
  transfers between devices with their start and end apart: 1, of which 1 were waited for; matrix products, arithmetic and copies ran while one was open for 0% of the time, Pallas kernels for 0%

commit v1 on v0

v1 whole, which is shorter than its diff:
```python
import functools

import jax
import jax.numpy as jnp
from jax import lax
from jax.experimental import pallas as pl
from jax.experimental.pallas import tpu as pltpu
from jax.sharding import PartitionSpec as P

LANES = 128
RING = 6
LEAD = 3
LAG = 4
DIRECT = 2
PIECES = 2
LOG2E = 1.4426950408889634


def kernel(n, groups, q_hbm, k_hbm, v_hbm, out, q_in, spread, mask, q_wide, keys, values, weights, parts, stats, round_parts, round_stats, last_parts, last_stats,
           q_sem, k_sems, v_sems, tail_sems, part_send, stat_send, out_send, part_recv, stat_recv, out_recv, last_send, last_recv):
    sequences, width, _ = k_hbm.shape
    rows, head = q_hbm.shape
    heads = rows // sequences
    share = heads // groups
    last = sequences - 1
    shared = sequences - DIRECT
    piece = width // PIECES
    me = lax.axis_index("sp")
    peers = [{"sp": lax.rem(me + step, n)} for step in range(1, n)]

    def k_copy(i):
        return pltpu.make_async_copy(k_hbm.at[i], keys.at[lax.rem(i, RING)], k_sems.at[lax.rem(i, RING)])

    def v_copy(i):
        return pltpu.make_async_copy(v_hbm.at[i], values.at[lax.rem(i, RING)], v_sems.at[lax.rem(i, RING)])

    def tail_copy(p):
        at = pl.ds(piece * p, piece)
        return pltpu.make_async_copy(v_hbm.at[last, at], values.at[last % RING, at], tail_sems.at[p])

    def start_k(i):
        if isinstance(i, int):
            k_copy(i).start()
        else:
            pl.when(i < sequences)(lambda: k_copy(i).start())

    def start_v(i):
        if isinstance(i, int):
            v_copy(i).start()
            return
        pl.when(i < last)(lambda: v_copy(i).start())

        @pl.when(i == last)
        def _():
            for p in range(PIECES):
                tail_copy(p).start()

    def push(src, dst, send_sem, recv_sem, peer):
        pltpu.make_async_remote_copy(
            src_ref=src, dst_ref=dst, send_sem=send_sem, recv_sem=recv_sem, device_id=peer, device_id_type=pl.DeviceIdType.MESH
        ).start()

    def wait_for(ref, sem):
        pltpu.make_async_copy(ref, ref, sem).wait()

    def slot_of(i):
        return lax.rem(me - lax.rem(i, n) + n, n)

    def to_owner(i, src, dst, send_sem, recv_sem):
        slot = slot_of(i)

        @pl.when(slot > 0)
        def _():
            push(src.at[i], dst.at[lax.div(i, n), slot - 1], send_sem.at[i], recv_sem.at[lax.div(i, n)], {"sp": lax.rem(i, n)})

    def sent_to_owner(i, src, send_sem):
        pl.when(slot_of(i) > 0)(lambda: wait_for(src.at[i], send_sem.at[i]))

    def send_stats(i):
        to_owner(i, stats, round_stats, stat_send, stat_recv)

    def send_parts(i):
        to_owner(i, parts, round_parts, part_send, part_recv)

    def to_all(src, send_sem, recv_sem):
        for peer in peers:
            push(src, src, send_sem, recv_sem, peer)

    def tail_of(p):
        return pl.ds(heads // PIECES * p, heads // PIECES), last_send.at[DIRECT - 1 + p], last_recv.at[DIRECT - 1 + p]

    q_copy = pltpu.make_async_copy(q_hbm, q_in, q_sem)
    q_copy.start()
    for i in range(LEAD):
        k_copy(i).start()
    for i in range(LEAD, RING):
        k_copy(i).start()
        v_copy(i - LEAD).start()

    barrier = pltpu.get_barrier_semaphore()
    for peer in peers:
        pl.semaphore_signal(barrier, inc=1, device_id=peer, device_id_type=pl.DeviceIdType.MESH)

    column = lax.broadcasted_iota(jnp.int32, (8, width), 1)
    group = sum((column >= head * g).astype(jnp.int32) for g in range(1, groups))
    place = jnp.broadcast_to((column - head * group)[:1], (head, width))
    spread[...] = (lax.broadcasted_iota(jnp.int32, (head, width), 0) == place).astype(jnp.float32).astype(jnp.bfloat16)
    row = lax.broadcasted_iota(jnp.int32, (heads, width), 0) - share * jnp.broadcast_to(group[:1], (heads, width))
    mask[...] = jnp.logical_and(row >= 0, row < share).astype(jnp.float32).astype(jnp.bfloat16)

    q_copy.wait()
    few = 4 * heads

    def widen(i, _):
        at = pl.ds(pl.multiple_of(i * few, few), few)
        wide = jnp.dot(q_in[at, :], spread[...], preferred_element_type=jnp.float32).astype(jnp.bfloat16)
        q_wide[at, :] = wide * jnp.concatenate([mask[...]] * 4, 0)
        return 0

    lax.fori_loop(0, rows // few, widen, 0)

    lane = lax.broadcasted_iota(jnp.int32, (heads, LANES), 1)
    line = lax.broadcasted_iota(jnp.int32, (heads, LANES), 0)
    row8 = lax.broadcasted_iota(jnp.int32, (8, LANES), 0)
    factor = head**-0.5

    def weigh(i, direct=False):
        at = pl.ds(pl.multiple_of(i * heads, heads), heads)
        raw = jnp.dot(q_wide[at, :], keys[lax.rem(i, RING)], preferred_element_type=jnp.float32)
        high = jnp.max(raw, -1, keepdims=True)
        w = jnp.exp2((raw - high) * (factor * LOG2E))
        weights[lax.rem(i, LEAD + 1)] = w.astype(jnp.bfloat16)
        total = jnp.sum(w, -1, keepdims=True)
        both = jnp.where(lane == line, high * factor, 0.0) + jnp.where(lane == line + heads, total, 0.0)
        both = jnp.broadcast_to(jnp.sum(both, 0, keepdims=True), (8, LANES))
        if direct:
            last_stats[i - shared, me] = jnp.where(row8 == me, both, 0.0)
        else:
            stats[i] = jnp.where(row8 == slot_of(i), both, 0.0)

    def gather(i, w, first=0, count=None, direct=False):
        count = heads if count is None else count
        start = head * (first // share)
        size = head * (count // share)
        seen = lax.dot_general(
            w[first : first + count], values[lax.rem(i, RING), start : start + size], (((1,), (1,)), ((), ())), preferred_element_type=jnp.float32
        )
        upper = lax.broadcasted_iota(jnp.int32, (8, 2 * LANES), 0)
        blocks = []
        for top in range(0, count, 8):
            block = None
            for g in range(top // share, (top + 8) // share):
                begin = head * g
                base = min(begin // LANES * LANES, -(-size // LANES) * LANES - 2 * LANES)
                part = seen[top : top + 8, base : min(base + 2 * LANES, size)]
                if part.shape[1] < 2 * LANES:
                    part = jnp.concatenate([part, jnp.zeros((8, 2 * LANES - part.shape[1]), part.dtype)], 1)
                if begin > base:
                    part = pltpu.roll(part, 2 * LANES - (begin - base), 1)
                block = part if block is None else jnp.where(upper >= share * g - top, part, block)
            blocks.append(block)
        found = jnp.concatenate(blocks, 0).astype(jnp.bfloat16)
        if direct:
            last_parts[i - shared, me, first : first + count] = found
        else:
            parts[i] = found

    def scales(found):
        found = functools.reduce(lax.add, found)
        scale = jnp.exp(found - jnp.max(found, 0, keepdims=True))
        total = jnp.sum(pltpu.roll(found, LANES - heads, 1) * scale, 0, keepdims=True)
        scale = scale / total
        return [
            jnp.sum(jnp.where(lane == line, jnp.broadcast_to(scale[d : d + 1], (heads, LANES)), 0.0), -1, keepdims=True)
            for d in range(n)
        ]

    def join(i, factors, found):
        result = jnp.zeros((heads, 2 * LANES), jnp.float32)
        for d in range(n):
            result = result + found[d].astype(jnp.float32) * factors[d]
        out[i] = result[:, :head].astype(out.dtype)

    def join_own(r):
        i = n * r + me
        wait_for(round_stats.at[r], stat_recv.at[r])
        factors = scales([stats[i]] + [round_stats[r, d] for d in range(n - 1)])
        wait_for(round_parts.at[r], part_recv.at[r])
        join(i, factors, [parts[i]] + [round_parts[r, d] for d in range(n - 1)])
        to_all(out.at[i], out_send.at[r], out_recv.at[r])

    for i in range(LEAD):
        k_copy(i).wait()
        weigh(i)
        start_k(i + RING)
        start_v(i + RING - LEAD)
    pl.semaphore_wait(barrier, n - 1)
    for i in range(LEAD - 1):
        send_stats(i)

    def step(i, follows=True, direct=False, first=False):
        if follows:
            start_k(i + LEAD + RING - 1)
            start_v(i + RING - 1)

            @pl.when(jnp.logical_and(lax.rem(i, n) == LAG, i > n))
            def _():
                join_own(lax.div(i, n) - 1)

            send_parts(i - 1)
        k_copy(i + LEAD).wait()
        v_copy(i).wait()
        if not direct or first:
            send_stats(i + LEAD - 1)
        w = weights[lax.rem(i, LEAD + 1)]
        weigh(i + LEAD, direct)
        gather(i, w)

    def body(i, _):
        step(i)
        return 0

    step(0, follows=False)
    lax.fori_loop(1, shared - LEAD, body, 0)
    for i in range(shared - LEAD, sequences - LEAD):
        step(jnp.int32(i), direct=True, first=i == shared - LEAD)
        to_all(last_stats.at[i + LEAD - shared, me], stat_send.at[i + LEAD], last_recv.at[DIRECT + PIECES - 1 + i + LEAD - shared])

    send_parts(last - LEAD)
    for i in range(sequences - LEAD, last):
        v_copy(i).wait()
        gather(i, weights[i % (LEAD + 1)], direct=i >= shared)
        if i < shared:
            send_parts(i)
        else:
            to_all(last_parts.at[i - shared, me], last_send.at[i - shared], last_recv.at[i - shared])
    w = weights[last % (LEAD + 1)]
    for p in range(PIECES):
        tail_copy(p).wait()
        gather(last, w, heads // PIECES * p, heads // PIECES, direct=True)
        at, send_sem, recv_sem = tail_of(p)
        to_all(last_parts.at[DIRECT - 1, me, at], send_sem, recv_sem)

    rounds = -(-shared // n)
    owners = shared - n * (rounds - 1)
    pl.when(me < owners)(lambda: join_own(rounds - 1))

    for i in range(shared, last):
        d = i - shared
        wait_for(last_stats.at[d, pl.ds(0, n - 1)], last_recv.at[DIRECT + PIECES - 1 + d])
        factors = scales([last_stats[d, e] for e in range(n)])
        wait_for(last_parts.at[d, pl.ds(0, n - 1)], last_recv.at[d])
        join(i, factors, [last_parts[d, e] for e in range(n)])
    d = DIRECT - 1
    wait_for(last_stats.at[d, pl.ds(0, n - 1)], last_recv.at[DIRECT + PIECES - 1 + d])
    factors = scales([last_stats[d, e] for e in range(n)])
    for p in range(PIECES):
        at, send_sem, recv_sem = tail_of(p)
        wait_for(last_parts.at[d, pl.ds(0, n - 1), at], recv_sem)
    join(last, factors, [last_parts[d, e] for e in range(n)])

    def drain(i, _):
        sent_to_owner(i, stats, stat_send)
        sent_to_owner(i, parts, part_send)
        return 0

    lax.fori_loop(0, shared, drain, 0)
    for i in range(shared, sequences):
        wait_for(last_stats.at[i - shared, pl.ds(0, n - 1)], stat_send.at[i])
        if i < last:
            wait_for(last_parts.at[i - shared, pl.ds(0, n - 1)], last_send.at[i - shared])
    for p in range(PIECES):
        at, send_sem, recv_sem = tail_of(p)
        wait_for(last_parts.at[DIRECT - 1, pl.ds(0, n - 1), at], send_sem)
    for r in range(rounds):
        each = n if r < rounds - 1 else owners

        @pl.when(me < each)
        def _():
            wait_for(out.at[pl.ds(n * r, n - 1)], out_send.at[r])
            wait_for(out.at[pl.ds(n * r, each - 1)], out_recv.at[r])

        @pl.when(me >= each)
        def _():
            wait_for(out.at[pl.ds(n * r, each)], out_recv.at[r])


def attend(n, q, k, v):
    sequences, heads, head = q.shape
    tokens, groups = k.shape[1:3]
    width = groups * head
    rounds = -(-(sequences - DIRECT) // n)
    k, v = (jnp.transpose(x, (0, 2, 3, 1)).reshape(sequences, width, tokens) for x in (k, v))
    return pl.pallas_call(
        functools.partial(kernel, n, groups),
        out_shape=pltpu.VMEM(q.shape, q.dtype),
        in_specs=[pl.BlockSpec(memory_space=pl.ANY)] * 3,
        out_specs=pl.BlockSpec(memory_space=pltpu.VMEM),
        scratch_shapes=[
            pltpu.VMEM((sequences * heads, head), jnp.bfloat16),
            pltpu.VMEM((head, width), jnp.bfloat16),
            pltpu.VMEM((heads, width), jnp.bfloat16),
            pltpu.VMEM((sequences * heads, width), jnp.bfloat16),
            pltpu.VMEM((RING, width, tokens), jnp.bfloat16),
            pltpu.VMEM((RING, width, tokens), jnp.bfloat16),
            pltpu.VMEM((LEAD + 1, heads, tokens), jnp.bfloat16),
            pltpu.VMEM((sequences - DIRECT, heads, 2 * LANES), jnp.bfloat16),
            pltpu.VMEM((sequences - DIRECT, 8, LANES), jnp.float32),
            pltpu.VMEM((rounds, n - 1, heads, 2 * LANES), jnp.bfloat16),
            pltpu.VMEM((rounds, n - 1, 8, LANES), jnp.float32),
            pltpu.VMEM((DIRECT, n, heads, 2 * LANES), jnp.bfloat16),
            pltpu.VMEM((DIRECT, n, 8, LANES), jnp.float32),
            pltpu.SemaphoreType.DMA,
            pltpu.SemaphoreType.DMA((RING,)),
            pltpu.SemaphoreType.DMA((RING,)),
            pltpu.SemaphoreType.DMA((PIECES,)),
            pltpu.SemaphoreType.DMA((sequences,)),
            pltpu.SemaphoreType.DMA((sequences,)),
            pltpu.SemaphoreType.DMA((rounds,)),
            pltpu.SemaphoreType.DMA((rounds,)),
            pltpu.SemaphoreType.DMA((rounds,)),
            pltpu.SemaphoreType.DMA((rounds,)),
            pltpu.SemaphoreType.DMA((DIRECT + PIECES - 1,)),
            pltpu.SemaphoreType.DMA((2 * DIRECT + PIECES - 1,)),
        ],
        compiler_params=pltpu.CompilerParams(collective_id=0, has_side_effects=True, vmem_limit_bytes=56 * 2**20),
        name="attend",
    )(q.reshape(sequences * heads, head), k, v)


def solution(mesh):
    return jax.shard_map(
        functools.partial(attend, mesh.shape["sp"]),
        mesh=mesh,
        in_specs=(P("dp", None, None), P("dp", "sp", None, None), P("dp", "sp", None, None)),
        out_specs=P("dp", None, None),
        check_vma=False,
    )
```

time: 158 us -> 66.4 us (0.42)
  Pallas kernels: 0 us -> 65.5 us
  matrix products: 62.1 us -> 0 us
  waiting for transfers between devices: 49 us -> 0 us
  other arithmetic: 17.6 us -> 0 us
  local copies, waits for them, and re-layouts: 15.2 us -> 0.8 us
  between operations: 13.5 us -> 0.01 us
    pallas_call x0 -> x1, Pallas kernels: none -> 65.5 us  [attend(): pl.pallas_call(functools.partial(kernel, n, groups), out_shape=pltpu.VMEM...]
    dot_general x2 -> x0, matrix products: 62.1 us -> none  [einsum(): return jnp.einsum(form, a.astype(jnp.float32), b.astype(jnp.float32))]
    all_gather x1 -> x0, waiting for transfers between devices: 48.9 us -> none  [step(): return together(lax.all_gather(part_of(q, k, v), 'sp')).reshape(q.shape)]
    slice x1 -> x0, other arithmetic: 8.92 us -> none  [together(): seen, total, high = (parts[..., :-2], parts[..., -2:-1], parts[..., -1:])]
    reduce_sum x3 -> x0, other arithmetic: 7.82 us -> none  [the longest x1 4.16 us: together(): jnp.sum(seen * scale, 0) / jnp.sum(total * scale, 0)]
    unnamed x3 -> x1, local copies, waits for them, and re-layouts: 7.41 us -> 0.8 us
    broadcast_in_dim x2 -> x0, local copies, waits for them, and re-layouts: 3.33 us -> none  [the longest x1 1.66 us: part_of(): jnp.sum(weights, -1, keepdims=True)]
  transfers between devices with their start and end apart: 1 -> 0, of which waited for: 1 -> 0; matrix products, arithmetic and copies ran while one was open for 0% -> 0% of each run, Pallas kernels for 0% -> 0%
where the time goes in v1:
time: 66.4 us; the launch traced here: 66.3 us
  Pallas kernels  65.5 us (99%)
  local copies, waits for them, and re-layouts  0.8 us (1%)
    pallas_call x1, Pallas kernels, attend(): pl.pallas_call(functools.partial(kernel, n, groups), out_shape=pltpu.VMEM...  65.5 us

profile of v1, /device:TPU:113, one launch (start us, length us, event | category | flops | bytes accessed | tf_op | source)
XLA Modules:
  0.0 66.3 jit_solution(17016095112017178553)
XLA Ops:
  0.0 65.5 %attend.1 = bf16[32,32,160]{2,1,0:T(8,128)(2,1)S(1)} custom-call(bf16[1024,160]{1,0:T(8,128)(2,1)} %bitcast.7, bf16[32,1280,1024]{2,1,0:T(8,128)(2,1)} %bitcast.2.k_hbm, bf16[32,1280,1024]{2,1,0:T(8,128)(2,1)} %bitcast.4.v_hbm), custom_call_target="tpu_custom_call" | custom-call | tf_op jit(solution)/shard_map/attend/pallas_call | solution.py:294
  65.5 0.8 %copy.5 = bf16[32,32,160]{2,1,0:T(8,128)(2,1)} copy(bf16[32,32,160]{2,1,0:T(8,128)(2,1)S(1)} %attend.1) | data formatting | bytes 655360

commit v2 on v1

v2 whole, which is shorter than its diff:
```python
import functools

import jax
import jax.numpy as jnp
from jax import lax
from jax.experimental import pallas as pl
from jax.experimental.pallas import tpu as pltpu
from jax.sharding import PartitionSpec as P

LANES = 128
RING = 6
LEAD = 1
LAG = 3
DIRECT = 3
PIECES = 2
LOG2E = 1.4426950408889634


def kernel(n, groups, q_hbm, k_hbm, v_hbm, out, q_in, spread, mask, q_wide, keys, values, weights, parts, stats, round_parts, round_stats, last_parts, last_stats,
           q_sem, k_sems, v_sems, tail_sems, part_send, stat_send, out_send, part_recv, stat_recv, out_recv, last_send, last_recv, last_stat_send, last_stat_recv):
    sequences, width, _ = k_hbm.shape
    rows, head = q_hbm.shape
    heads = rows // sequences
    share = heads // groups
    last = sequences - 1
    shared = sequences - DIRECT
    piece = width // PIECES
    few = heads // PIECES
    rest = head - LANES
    me = lax.axis_index("sp")
    peers = [{"sp": lax.rem(me + step, n)} for step in range(1, n)]

    def k_copy(i):
        return pltpu.make_async_copy(k_hbm.at[i], keys.at[lax.rem(i, RING)], k_sems.at[lax.rem(i, RING)])

    def v_copy(i):
        return pltpu.make_async_copy(v_hbm.at[i], values.at[lax.rem(i, RING)], v_sems.at[lax.rem(i, RING)])

    def tail_copy(p):
        at = pl.ds(piece * p, piece)
        return pltpu.make_async_copy(v_hbm.at[last, at], values.at[last % RING, at], tail_sems.at[p])

    def start_k(i):
        if not isinstance(i, int):
            pl.when(i < sequences)(lambda: k_copy(i).start(priority=1))
        elif i < sequences:
            k_copy(i).start(priority=1)

    def start_v(i):
        def whole():
            v_copy(i).start(priority=1)

        def pieces():
            for p in range(PIECES):
                tail_copy(p).start(priority=1)

        if not isinstance(i, int):
            pl.when(i < last)(whole)
            pl.when(i == last)(pieces)
        elif i <= last:
            (whole if i < last else pieces)()

    def push(src, dst, send_sem, recv_sem, peer):
        pltpu.make_async_remote_copy(
            src_ref=src, dst_ref=dst, send_sem=send_sem, recv_sem=recv_sem, device_id=peer, device_id_type=pl.DeviceIdType.MESH
        ).start()

    def wait_for(ref, sem):
        pltpu.make_async_copy(ref, ref, sem).wait()

    def slot_of(i):
        return lax.rem(me - lax.rem(i, n) + n, n)

    def to_owner(i, src, dst, send_sem, recv_sem):
        slot = slot_of(i)
        r = lax.div(i, n)

        @pl.when(slot > 0)
        def _():
            push(src.at[i], dst.at[r, slot - 1], send_sem.at[r], recv_sem.at[r], {"sp": lax.rem(i, n)})

    def send_stats(i):
        if isinstance(i, int) and i >= shared:
            to_all(last_stats.at[i - shared, me], last_stat_send.at[i - shared], last_stat_recv.at[i - shared])
        else:
            to_owner(i, stats, round_stats, stat_send, stat_recv)

    def send_parts(i):
        if isinstance(i, int) and i >= shared:
            to_all(last_parts.at[i - shared, me], last_send.at[i - shared], last_recv.at[i - shared])
        else:
            to_owner(i, parts, round_parts, part_send, part_recv)

    def to_all(src, send_sem, recv_sem):
        for peer in peers:
            push(src, src, send_sem, recv_sem, peer)

    def tail_of(p):
        return last_send.at[DIRECT - 1 + p], last_recv.at[DIRECT - 1 + p]

    q_copy = pltpu.make_async_copy(q_hbm, q_in, q_sem)
    q_copy.start()
    for i in range(LEAD):
        k_copy(i).start(priority=1)
    for i in range(LEAD, RING):
        k_copy(i).start(priority=1)
        v_copy(i - LEAD).start(priority=1)

    barrier = pltpu.get_barrier_semaphore()
    for peer in peers:
        pl.semaphore_signal(barrier, inc=1, device_id=peer, device_id_type=pl.DeviceIdType.MESH)

    column = lax.broadcasted_iota(jnp.int32, (8, width), 1)
    group = sum((column >= head * g).astype(jnp.int32) for g in range(1, groups))
    place = jnp.broadcast_to((column - head * group)[:1], (head, width))
    spread[...] = (lax.broadcasted_iota(jnp.int32, (head, width), 0) == place).astype(jnp.float32).astype(jnp.bfloat16)
    row = lax.broadcasted_iota(jnp.int32, (heads, width), 0) - share * jnp.broadcast_to(group[:1], (heads, width))
    mask[...] = jnp.logical_and(row >= 0, row < share).astype(jnp.float32).astype(jnp.bfloat16)

    q_copy.wait()
    many = 4 * heads

    def widen(i, _):
        at = pl.ds(pl.multiple_of(i * many, many), many)
        wide = jnp.dot(q_in[at, :], spread[...], preferred_element_type=jnp.float32).astype(jnp.bfloat16)
        q_wide[at, :] = wide * jnp.concatenate([mask[...]] * 4, 0)
        return 0

    lax.fori_loop(0, rows // many, widen, 0)

    lane = lax.broadcasted_iota(jnp.int32, (heads, LANES), 1)
    line = lax.broadcasted_iota(jnp.int32, (heads, LANES), 0)
    row8 = lax.broadcasted_iota(jnp.int32, (8, LANES), 0)
    lane8 = lax.broadcasted_iota(jnp.int32, (8, LANES), 1)
    factor = head**-0.5

    def weigh(i):
        direct = isinstance(i, int) and i >= shared
        at = pl.ds(pl.multiple_of(i * heads, heads), heads)
        raw = jnp.dot(q_wide[at, :], keys[lax.rem(i, RING)], preferred_element_type=jnp.float32)
        high = jnp.max(raw, -1, keepdims=True)
        w = jnp.exp2((raw - high) * (factor * LOG2E))
        weights[lax.rem(i, LEAD + 1)] = w.astype(jnp.bfloat16)
        total = jnp.sum(w, -1, keepdims=True)
        both = jnp.where(lane == line, high * factor, 0.0) + jnp.where(lane == line + heads, total, 0.0)
        both = jnp.sum(both, 0, keepdims=True)
        if direct:
            last_stats[i - shared, me] = both
        else:
            stats[i] = jnp.where(row8 == slot_of(i), jnp.broadcast_to(both, (8, LANES)), 0.0)

    def gather(i, w, first=0, count=None):
        count = heads if count is None else count
        start = head * (first // share)
        size = head * (count // share)
        seen = lax.dot_general(
            w[first : first + count], values[lax.rem(i, RING), start : start + size], (((1,), (1,)), ((), ())), preferred_element_type=jnp.float32
        )
        upper = lax.broadcasted_iota(jnp.int32, (8, 2 * LANES), 0)
        blocks = []
        for top in range(0, count, 8):
            block = None
            for g in range(top // share, (top + 8) // share):
                begin = head * g
                base = min(begin // LANES * LANES, -(-size // LANES) * LANES - 2 * LANES)
                part = seen[top : top + 8, base : min(base + 2 * LANES, size)]
                if part.shape[1] < 2 * LANES:
                    part = jnp.concatenate([part, jnp.zeros((8, 2 * LANES - part.shape[1]), part.dtype)], 1)
                if begin > base:
                    part = pltpu.roll(part, 2 * LANES - (begin - base), 1)
                block = part if block is None else jnp.where(upper >= share * g - top, part, block)
            blocks.append(block)
        if isinstance(i, int) and i >= shared:
            for p in range(count // few):
                pack = pack_rows(blocks[few // 8 * p : few // 8 * (p + 1)])
                last_parts[i - shared, me, first // few + p] = pack.astype(jnp.bfloat16)
        else:
            parts[i] = jnp.concatenate(blocks, 0).astype(jnp.bfloat16)

    def pack_rows(blocks):
        over = blocks[0][:, LANES:]
        for j, block in enumerate(blocks[1:], 1):
            over = jnp.where(lane8 >= rest * j, pltpu.roll(block[:, LANES:], rest * j, 1), over)
        return jnp.concatenate([block[:, :LANES] for block in blocks] + [over], 0)

    def join_packed(i, factors):
        for p in range(PIECES):
            result = jnp.zeros((few + 8, LANES), jnp.float32)
            for e in range(n):
                weight = jnp.broadcast_to(factors[e][few * p : few * (p + 1)], (few, LANES))
                blocks = [weight[8 * j : 8 * j + 8] for j in range(few // 8)]
                over = blocks[0]
                for j, block in enumerate(blocks[1:], 1):
                    over = jnp.where(lane8 >= rest * j, block, over)
                result = result + last_parts[i - shared, e, p].astype(jnp.float32) * jnp.concatenate(blocks + [over], 0)
            out[i, few * p : few * (p + 1), :LANES] = result[:few].astype(out.dtype)
            over = [result[few:]] + [pltpu.roll(result[few:], LANES - rest * j, 1) for j in range(1, few // 8)]
            out[i, few * p : few * (p + 1), LANES:] = jnp.concatenate(over, 0)[:, :rest].astype(out.dtype)

    def last_scales(d):
        return scales([jnp.where(row8 == e, jnp.broadcast_to(last_stats[d, e], (8, LANES)), 0.0) for e in range(n)])

    def scales(found):
        found = functools.reduce(lax.add, found)
        scale = jnp.exp(found - jnp.max(found, 0, keepdims=True))
        total = jnp.sum(pltpu.roll(found, LANES - heads, 1) * scale, 0, keepdims=True)
        scale = scale / total
        return [
            jnp.sum(jnp.where(lane == line, jnp.broadcast_to(scale[d : d + 1], (heads, LANES)), 0.0), -1, keepdims=True)
            for d in range(n)
        ]

    def join(i, factors, found):
        result = jnp.zeros((heads, 2 * LANES), jnp.float32)
        for d in range(n):
            result = result + found[d].astype(jnp.float32) * factors[d]
        out[i] = result[:, :head].astype(out.dtype)

    def join_own(r):
        i = n * r + me
        wait_for(round_stats.at[r], stat_recv.at[r])
        factors = scales([stats[i]] + [round_stats[r, d] for d in range(n - 1)])
        wait_for(round_parts.at[r], part_recv.at[r])
        join(i, factors, [parts[i]] + [round_parts[r, d] for d in range(n - 1)])
        to_all(out.at[i], out_send.at[r], out_recv.at[r])

    for i in range(LEAD):
        k_copy(i).wait()
        weigh(i)
        start_k(i + RING)
        start_v(i + RING - LEAD)
    pl.semaphore_wait(barrier, n - 1)
    for i in range(LEAD - 1):
        send_stats(i)

    def step(i, first=False):
        if not first:
            start_k(i + LEAD + RING - 1)
            start_v(i + RING - 1)
            if not isinstance(i, int):
                pl.when(jnp.logical_and(lax.rem(i, n) == LAG, i > n))(lambda: join_own(lax.div(i, n) - 1))
            elif i % n == LAG and i > n:
                join_own(i // n - 1)
            send_parts(i - 1)
        send_stats(i + LEAD - 1)
        k_copy(i + LEAD).wait()
        v_copy(i).wait()
        w = weights[lax.rem(i, LEAD + 1)]
        weigh(i + LEAD)
        gather(i, w)

    def body(i, _):
        step(i)
        return 0

    step(0, first=True)
    lax.fori_loop(1, shared - LEAD, body, 0)
    for i in range(shared - LEAD, sequences - LEAD):
        step(i)

    send_stats(last)
    send_parts(last - LEAD)
    for i in range(sequences - LEAD, last):
        v_copy(i).wait()
        gather(i, weights[i % (LEAD + 1)])
        send_parts(i)
    w = weights[last % (LEAD + 1)]
    for p in range(PIECES):
        tail_copy(p).wait()
        gather(last, w, few * p, few)
        to_all(last_parts.at[DIRECT - 1, me, p], *tail_of(p))

    rounds = -(-shared // n)
    owners = shared - n * (rounds - 1)
    pl.when(me < owners)(lambda: join_own(rounds - 1))

    def each_round(r, own, other):
        if n * (r + 1) <= shared:
            own(n)
        else:
            pl.when(me < owners)(lambda: own(owners))
            pl.when(me >= owners)(lambda: other(owners))

    for r in range(rounds):

        def sent(count):
            if count:
                wait_for(stats.at[pl.ds(n * r, count)], stat_send.at[r])
                wait_for(parts.at[pl.ds(n * r, count)], part_send.at[r])

        each_round(r, lambda count: sent(count - 1), sent)
    for d in range(DIRECT):
        wait_for(last_stats.at[d, pl.ds(0, n - 1)], last_stat_send.at[d])

    for d in range(DIRECT - 1):
        wait_for(last_stats.at[d, pl.ds(0, n - 1)], last_stat_recv.at[d])
        factors = last_scales(d)
        wait_for(last_parts.at[d, pl.ds(0, n - 1)], last_send.at[d])
        wait_for(last_parts.at[d, pl.ds(0, n - 1)], last_recv.at[d])
        join_packed(shared + d, factors)
    d = DIRECT - 1
    wait_for(last_stats.at[d, pl.ds(0, n - 1)], last_stat_recv.at[d])
    factors = last_scales(d)
    for p in range(PIECES):
        for sem in tail_of(p):
            wait_for(last_parts.at[d, pl.ds(0, n - 1), p], sem)
    join_packed(last, factors)

    for r in range(rounds):

        def sent(count):
            wait_for(out.at[pl.ds(0, n - 1)], out_send.at[r])
            wait_for(out.at[pl.ds(0, count - 1)], out_recv.at[r])

        each_round(r, sent, lambda count: wait_for(out.at[pl.ds(0, count)], out_recv.at[r]))


def attend(n, q, k, v):
    sequences, heads, head = q.shape
    tokens, groups = k.shape[1:3]
    width = groups * head
    rounds = -(-(sequences - DIRECT) // n)
    k, v = (jnp.transpose(x, (0, 2, 3, 1)).reshape(sequences, width, tokens) for x in (k, v))
    return pl.pallas_call(
        functools.partial(kernel, n, groups),
        out_shape=pltpu.VMEM(q.shape, q.dtype),
        in_specs=[pl.BlockSpec(memory_space=pl.ANY)] * 3,
        out_specs=pl.BlockSpec(memory_space=pltpu.VMEM),
        scratch_shapes=[
            pltpu.VMEM((sequences * heads, head), jnp.bfloat16),
            pltpu.VMEM((head, width), jnp.bfloat16),
            pltpu.VMEM((heads, width), jnp.bfloat16),
            pltpu.VMEM((sequences * heads, width), jnp.bfloat16),
            pltpu.VMEM((RING, width, tokens), jnp.bfloat16),
            pltpu.VMEM((RING, width, tokens), jnp.bfloat16),
            pltpu.VMEM((LEAD + 1, heads, tokens), jnp.bfloat16),
            pltpu.VMEM((sequences - DIRECT, heads, 2 * LANES), jnp.bfloat16),
            pltpu.VMEM((sequences - DIRECT, 8, LANES), jnp.float32),
            pltpu.VMEM((rounds, n - 1, heads, 2 * LANES), jnp.bfloat16),
            pltpu.VMEM((rounds, n - 1, 8, LANES), jnp.float32),
            pltpu.VMEM((DIRECT, n, PIECES, heads // PIECES + 8, LANES), jnp.bfloat16),
            pltpu.VMEM((DIRECT, n, 1, LANES), jnp.float32),
            pltpu.SemaphoreType.DMA,
            pltpu.SemaphoreType.DMA((RING,)),
            pltpu.SemaphoreType.DMA((RING,)),
            pltpu.SemaphoreType.DMA((PIECES,)),
            *[pltpu.SemaphoreType.DMA((rounds,))] * 6,
            *[pltpu.SemaphoreType.DMA((DIRECT + PIECES - 1,))] * 2,
            *[pltpu.SemaphoreType.DMA((DIRECT,))] * 2,
        ],
        compiler_params=pltpu.CompilerParams(collective_id=0, has_side_effects=True, vmem_limit_bytes=56 * 2**20),
        name="attend",
    )(q.reshape(sequences * heads, head), k, v)


def solution(mesh):
    return jax.shard_map(
        functools.partial(attend, mesh.shape["sp"]),
        mesh=mesh,
        in_specs=(P("dp", None, None), P("dp", "sp", None, None), P("dp", "sp", None, None)),
        out_specs=P("dp", None, None),
        check_vma=False,
    )
```

time: 66.4 us -> 60.3 us (0.908)
  Pallas kernels: 65.5 us -> 59.4 us
    pallas_call x1, Pallas kernels: 65.5 us -> 59.4 us  [attend(): pl.pallas_call(functools.partial(kernel, n, groups), out_shape=pltpu.VMEM...]
where the time goes in v2:
time: 60.3 us; the launch traced here: 60.2 us
  Pallas kernels  59.4 us (99%)
  local copies, waits for them, and re-layouts  0.8 us (1%)
    pallas_call x1, Pallas kernels, attend(): pl.pallas_call(functools.partial(kernel, n, groups), out_shape=pltpu.VMEM...  59.4 us

profile of v2, /device:TPU:113, one launch (start us, length us, event | category | flops | bytes accessed | tf_op | source)
XLA Modules:
  0.0 60.2 jit_solution(11758588044157683205)
XLA Ops:
  0.0 59.4 %attend.1 = bf16[32,32,160]{2,1,0:T(8,128)(2,1)S(1)} custom-call(bf16[1024,160]{1,0:T(8,128)(2,1)} %bitcast.7, bf16[32,1280,1024]{2,1,0:T(8,128)(2,1)} %bitcast.2.k_hbm, bf16[32,1280,1024]{2,1,0:T(8,128)(2,1)} %bitcast.4.v_hbm), custom_call_target="tpu_custom_call" | custom-call | tf_op jit(solution)/shard_map/attend/pallas_call | solution.py:324
  59.4 0.8 %copy.5 = bf16[32,32,160]{2,1,0:T(8,128)(2,1)} copy(bf16[32,32,160]{2,1,0:T(8,128)(2,1)S(1)} %attend.1) | data formatting | bytes 655360

commit v3 on v2

--- a/solution.py
+++ b/solution.py
@@ -11,8 +11,8 @@
 RING = 6
 LEAD = 1
 LAG = 3
-DIRECT = 3
-PIECES = 2
+DIRECT = 4
+PIECES = 1
 LOG2E = 1.4426950408889634
 
 
@@ -24,11 +24,13 @@
     share = heads // groups
     last = sequences - 1
     shared = sequences - DIRECT
+    rounds = -(-shared // n)
+    owners = shared - n * (rounds - 1)
     piece = width // PIECES
     few = heads // PIECES
     rest = head - LANES
     me = lax.axis_index("sp")
-    peers = [{"sp": lax.rem(me + step, n)} for step in range(1, n)]
+    peers = [{"sp": lax.rem(me + step, n)} for step in sorted(range(1, n), key=lambda step: -min(step, n - step))]
 
     def k_copy(i):
         return pltpu.make_async_copy(k_hbm.at[i], keys.at[lax.rem(i, RING)], k_sems.at[lax.rem(i, RING)])
@@ -80,9 +82,9 @@
             push(src.at[i], dst.at[r, slot - 1], send_sem.at[r], recv_sem.at[r], {"sp": lax.rem(i, n)})
 
     def send_stats(i):
-        if isinstance(i, int) and i >= shared:
-            to_all(last_stats.at[i - shared, me], last_stat_send.at[i - shared], last_stat_recv.at[i - shared])
-        else:
+        if isinstance(i, int) and i == last:
+            to_all(last_stats.at[me], last_stat_send, last_stat_recv)
+        elif not isinstance(i, int) or i < shared:
             to_owner(i, stats, round_stats, stat_send, stat_recv)
 
     def send_parts(i):
@@ -145,43 +147,54 @@
         both = jnp.where(lane == line, high * factor, 0.0) + jnp.where(lane == line + heads, total, 0.0)
         both = jnp.sum(both, 0, keepdims=True)
         if direct:
-            last_stats[i - shared, me] = both
+            last_stats[me, i - shared] = both
         else:
             stats[i] = jnp.where(row8 == slot_of(i), jnp.broadcast_to(both, (8, LANES)), 0.0)
 
-    def gather(i, w, first=0, count=None):
-        count = heads if count is None else count
+    def gather(i, w, first=0, count=heads):
         start = head * (first // share)
         size = head * (count // share)
-        seen = lax.dot_general(
-            w[first : first + count], values[lax.rem(i, RING), start : start + size], (((1,), (1,)), ((), ())), preferred_element_type=jnp.float32
-        )
-        upper = lax.broadcasted_iota(jnp.int32, (8, 2 * LANES), 0)
-        blocks = []
-        for top in range(0, count, 8):
+        tokens = w.shape[1]
+        w = w[first : first + count]
+
+        def dot(begin, end, cut=slice(0, tokens)):
+            block = values[lax.rem(i, RING), start + begin : start + end, cut]
+            return lax.dot_general(w[:, cut], block, (((1,), (1,)), ((), ())), preferred_element_type=jnp.float32)
+
+        even = size // (4 * LANES) * (4 * LANES) if isinstance(i, int) and i == last else size
+        seen, more = dot(0, even), None
+        if even < size:
+            seen = jnp.concatenate([seen, dot(even, size, slice(0, tokens // 2))], 1)
+            more = dot(even, size, slice(tokens // 2, tokens))
+
+        def taken(top, shift_of):
             block = None
             for g in range(top // share, (top + 8) // share):
                 begin = head * g
-                base = min(begin // LANES * LANES, -(-size // LANES) * LANES - 2 * LANES)
-                part = seen[top : top + 8, base : min(base + 2 * LANES, size)]
-                if part.shape[1] < 2 * LANES:
-                    part = jnp.concatenate([part, jnp.zeros((8, 2 * LANES - part.shape[1]), part.dtype)], 1)
-                if begin > base:
-                    part = pltpu.roll(part, 2 * LANES - (begin - base), 1)
+                base = min(begin // LANES * LANES, size - 2 * LANES)
+                shift = shift_of(begin - base) % (2 * LANES)
+                part = seen[top : top + 8, base : base + 2 * LANES]
+                part = pltpu.roll(part, shift, 1) if shift else part
+                if base + 2 * LANES > even:
+                    extra = more[top : top + 8, max(base - even, 0) : base + 2 * LANES - even]
+                    if base < even:
+                        extra = jnp.concatenate([jnp.zeros((8, even - base), extra.dtype), extra], 1)
+                    part = part + (pltpu.roll(extra, shift, 1) if shift else extra)
                 block = part if block is None else jnp.where(upper >= share * g - top, part, block)
-            blocks.append(block)
+            return block
+
+        upper = lax.broadcasted_iota(jnp.int32, (8, 2 * LANES), 0)
+        tops = range(0, count, 8)
         if isinstance(i, int) and i >= shared:
             for p in range(count // few):
-                pack = pack_rows(blocks[few // 8 * p : few // 8 * (p + 1)])
-                last_parts[i - shared, me, first // few + p] = pack.astype(jnp.bfloat16)
+                blocks, over = [], None
+                for j, top in enumerate(tops[few // 8 * p : few // 8 * (p + 1)]):
+                    blocks.append(taken(top, lambda column: -column)[:, :LANES])
+                    beside = taken(top, lambda column: rest * j - column - LANES)[:, :LANES]
+                    over = beside if over is None else jnp.where(lane8 >= rest * j, beside, over)
+                last_parts[i - shared, me, first // few + p] = jnp.concatenate(blocks + [over], 0).astype(jnp.bfloat16)
         else:
-            parts[i] = jnp.concatenate(blocks, 0).astype(jnp.bfloat16)
-
-    def pack_rows(blocks):
-        over = blocks[0][:, LANES:]
-        for j, block in enumerate(blocks[1:], 1):
-            over = jnp.where(lane8 >= rest * j, pltpu.roll(block[:, LANES:], rest * j, 1), over)
-        return jnp.concatenate([block[:, :LANES] for block in blocks] + [over], 0)
+            parts[i] = jnp.concatenate([taken(top, lambda column: -column) for top in tops], 0).astype(jnp.bfloat16)
 
     def join_packed(i, factors):
         for p in range(PIECES):
@@ -198,7 +211,7 @@
             out[i, few * p : few * (p + 1), LANES:] = jnp.concatenate(over, 0)[:, :rest].astype(out.dtype)
 
     def last_scales(d):
-        return scales([jnp.where(row8 == e, jnp.broadcast_to(last_stats[d, e], (8, LANES)), 0.0) for e in range(n)])
+        return scales([jnp.where(row8 == e, jnp.broadcast_to(last_stats[e, d], (8, LANES)), 0.0) for e in range(n)])
 
     def scales(found):
         found = functools.reduce(lax.add, found)
@@ -270,8 +283,6 @@
         gather(last, w, few * p, few)
         to_all(last_parts.at[DIRECT - 1, me, p], *tail_of(p))
 
-    rounds = -(-shared // n)
-    owners = shared - n * (rounds - 1)
     pl.when(me < owners)(lambda: join_own(rounds - 1))
 
     def each_round(r, own, other):
@@ -289,17 +300,15 @@
                 wait_for(parts.at[pl.ds(n * r, count)], part_send.at[r])
 
         each_round(r, lambda count: sent(count - 1), sent)
-    for d in range(DIRECT):
-        wait_for(last_stats.at[d, pl.ds(0, n - 1)], last_stat_send.at[d])
+    for sem in (last_stat_send, last_stat_recv):
+        wait_for(last_stats.at[pl.ds(0, n - 1)], sem)
 
     for d in range(DIRECT - 1):
-        wait_for(last_stats.at[d, pl.ds(0, n - 1)], last_stat_recv.at[d])
         factors = last_scales(d)
         wait_for(last_parts.at[d, pl.ds(0, n - 1)], last_send.at[d])
         wait_for(last_parts.at[d, pl.ds(0, n - 1)], last_recv.at[d])
         join_packed(shared + d, factors)
     d = DIRECT - 1
-    wait_for(last_stats.at[d, pl.ds(0, n - 1)], last_stat_recv.at[d])
     factors = last_scales(d)
     for p in range(PIECES):
         for sem in tail_of(p):
@@ -339,14 +348,14 @@
             pltpu.VMEM((rounds, n - 1, heads, 2 * LANES), jnp.bfloat16),
             pltpu.VMEM((rounds, n - 1, 8, LANES), jnp.float32),
             pltpu.VMEM((DIRECT, n, PIECES, heads // PIECES + 8, LANES), jnp.bfloat16),
-            pltpu.VMEM((DIRECT, n, 1, LANES), jnp.float32),
+            pltpu.VMEM((n, DIRECT, 1, LANES), jnp.float32),
             pltpu.SemaphoreType.DMA,
             pltpu.SemaphoreType.DMA((RING,)),
             pltpu.SemaphoreType.DMA((RING,)),
             pltpu.SemaphoreType.DMA((PIECES,)),
             *[pltpu.SemaphoreType.DMA((rounds,))] * 6,
             *[pltpu.SemaphoreType.DMA((DIRECT + PIECES - 1,))] * 2,
-            *[pltpu.SemaphoreType.DMA((DIRECT,))] * 2,
+            *[pltpu.SemaphoreType.DMA] * 2,
         ],
         compiler_params=pltpu.CompilerParams(collective_id=0, has_side_effects=True, vmem_limit_bytes=56 * 2**20),
         name="attend",

time: 60.3 us -> 59.3 us (0.983)
  Pallas kernels: 59.4 us -> 58.4 us
    pallas_call x1, Pallas kernels: 59.4 us -> 58.4 us  [attend(): pl.pallas_call(functools.partial(kernel, n, groups), out_shape=pltpu.VMEM...]
where the time goes in v3:
time: 59.3 us; the launch traced here: 59.2 us
  Pallas kernels  58.4 us (98%)
  local copies, waits for them, and re-layouts  0.8 us (1%)
    pallas_call x1, Pallas kernels, attend(): pl.pallas_call(functools.partial(kernel, n, groups), out_shape=pltpu.VMEM...  58.4 us

profile of v3, /device:TPU:113, one launch (start us, length us, event | category | flops | bytes accessed | tf_op | source)
XLA Modules:
  0.0 59.2 jit_solution(7718172418335049191)
XLA Ops:
  0.0 58.4 %attend.1 = bf16[32,32,160]{2,1,0:T(8,128)(2,1)S(1)} custom-call(bf16[1024,160]{1,0:T(8,128)(2,1)} %bitcast.7, bf16[32,1280,1024]{2,1,0:T(8,128)(2,1)} %bitcast.2.k_hbm, bf16[32,1280,1024]{2,1,0:T(8,128)(2,1)} %bitcast.4.v_hbm), custom_call_target="tpu_custom_call" | custom-call | tf_op jit(solution)/shard_map/attend/pallas_call | solution.py:333
  58.4 0.8 %copy.5 = bf16[32,32,160]{2,1,0:T(8,128)(2,1)} copy(bf16[32,32,160]{2,1,0:T(8,128)(2,1)S(1)} %attend.1) | data formatting | bytes 655360

commit v4 on v3

--- a/solution.py
+++ b/solution.py
@@ -10,7 +10,7 @@
 LANES = 128
 RING = 6
 LEAD = 1
-LAG = 3
+LAG = 2
 DIRECT = 4
 PIECES = 1
 LOG2E = 1.4426950408889634
@@ -161,7 +161,7 @@
             block = values[lax.rem(i, RING), start + begin : start + end, cut]
             return lax.dot_general(w[:, cut], block, (((1,), (1,)), ((), ())), preferred_element_type=jnp.float32)
 
-        even = size // (4 * LANES) * (4 * LANES) if isinstance(i, int) and i == last else size
+        even = size // (4 * LANES) * (4 * LANES)
         seen, more = dot(0, even), None
         if even < size:
             seen = jnp.concatenate([seen, dot(even, size, slice(0, tokens // 2))], 1)

time: 59.3 us -> 59.3 us (level)
  no operation moved by 1% of the time
where the time goes in v4:
time: 59.3 us; the launch traced here: 59.2 us
  Pallas kernels  58.4 us (98%)
  local copies, waits for them, and re-layouts  0.8 us (1%)
    pallas_call x1, Pallas kernels, attend(): pl.pallas_call(functools.partial(kernel, n, groups), out_shape=pltpu.VMEM...  58.4 us

profile of v4, /device:TPU:113, one launch (start us, length us, event | category | flops | bytes accessed | tf_op | source)
XLA Modules:
  0.0 59.2 jit_solution(11115209901115026362)
XLA Ops:
  0.0 58.4 %attend.1 = bf16[32,32,160]{2,1,0:T(8,128)(2,1)S(1)} custom-call(bf16[1024,160]{1,0:T(8,128)(2,1)} %bitcast.7, bf16[32,1280,1024]{2,1,0:T(8,128)(2,1)} %bitcast.2.k_hbm, bf16[32,1280,1024]{2,1,0:T(8,128)(2,1)} %bitcast.4.v_hbm), custom_call_target="tpu_custom_call" | custom-call | tf_op jit(solution)/shard_map/attend/pallas_call | solution.py:333
  58.4 0.8 %copy.5 = bf16[32,32,160]{2,1,0:T(8,128)(2,1)} copy(bf16[32,32,160]{2,1,0:T(8,128)(2,1)S(1)} %attend.1) | data formatting | bytes 655360

commit v5 on v4

--- a/solution.py
+++ b/solution.py
@@ -254,6 +254,8 @@
                 pl.when(jnp.logical_and(lax.rem(i, n) == LAG, i > n))(lambda: join_own(lax.div(i, n) - 1))
             elif i % n == LAG and i > n:
                 join_own(i // n - 1)
+            elif i == last - LEAD:
+                pl.when(me < owners)(lambda: join_own(rounds - 1))
             send_parts(i - 1)
         send_stats(i + LEAD - 1)
         k_copy(i + LEAD).wait()
@@ -283,7 +285,6 @@
         gather(last, w, few * p, few)
         to_all(last_parts.at[DIRECT - 1, me, p], *tail_of(p))
 
-    pl.when(me < owners)(lambda: join_own(rounds - 1))
 
     def each_round(r, own, other):
         if n * (r + 1) <= shared:

time: 59.3 us -> 59.3 us (level)
  no operation moved by 1% of the time
where the time goes in v5:
time: 59.3 us; the launch traced here: 59.2 us
  Pallas kernels  58.4 us (98%)
  local copies, waits for them, and re-layouts  0.8 us (1%)
    pallas_call x1, Pallas kernels, attend(): pl.pallas_call(functools.partial(kernel, n, groups), out_shape=pltpu.VMEM...  58.4 us

profile of v5, /device:TPU:113, one launch (start us, length us, event | category | flops | bytes accessed | tf_op | source)
XLA Modules:
  0.0 59.2 jit_solution(12927114485070750689)
XLA Ops:
  0.0 58.4 %attend.1 = bf16[32,32,160]{2,1,0:T(8,128)(2,1)S(1)} custom-call(bf16[1024,160]{1,0:T(8,128)(2,1)} %bitcast.7, bf16[32,1280,1024]{2,1,0:T(8,128)(2,1)} %bitcast.2.k_hbm, bf16[32,1280,1024]{2,1,0:T(8,128)(2,1)} %bitcast.4.v_hbm), custom_call_target="tpu_custom_call" | custom-call | tf_op jit(solution)/shard_map/attend/pallas_call | solution.py:334
  58.4 0.8 %copy.5 = bf16[32,32,160]{2,1,0:T(8,128)(2,1)} copy(bf16[32,32,160]{2,1,0:T(8,128)(2,1)S(1)} %attend.1) | data formatting | bytes 655360
